TPU v7x, 256 devices: a 2x2x32 block of a 4x8x32 slice. The times are simulated.
256 devices in a mesh: groups: 4 (over x, y), seq: 64 (over z, core).
Axes of the slice: x: 2, y: 2, z: 32, core: 2. Of those that a mesh axis runs over, the one named last changes fastest.
The devices are a block of a 4x8x32 slice.
Arguments:
- img_query: bfloat16 [32, 512, 1536], P('groups', 'seq'), parts along dimension 0, may hold values from -13 to 13
- img_key: bfloat16 [32, 512, 1536], P('groups', 'seq'), parts along dimension 0, may hold values from -5 to 5
- img_value: bfloat16 [32, 512, 1536], P('groups', 'seq'), parts along dimension 0, may hold values from -5 to 5
- txt_key: bfloat16 [32, 256, 1536], P('groups', 'seq'), parts along dimension 0, may hold values from -5 to 5
- txt_value: bfloat16 [32, 256, 1536], P('groups', 'seq'), parts along dimension 0, may hold values from -5 to 5
- txt_len: int32 [32], P('groups'), parts along dimension 0, may hold values from 64 to 256
- slot_of: int32 [32], P('groups'), parts along dimension 0, may hold values from 0 to 7, each once
- step_index: int32 [4], P('groups'), parts along dimension 0, may hold values from 0 to 27
- residual: bfloat16 [32, 512, 1536], P('groups', 'seq'), parts along dimension 0, may hold values from -64 to 64
- modulation: float32 [32, 6, 1536], P('groups'), parts along dimension 0, may hold values from -4 to 4
- out_weight: bfloat16 [1536, 1536], replicated, may hold values from -0.15625 to 0.15625
- out_bias: float32 [1536], replicated, may hold values from -3 to 3
- expand_weight: bfloat16 [3072, 1536], P('seq'), may hold values from -0.15625 to 0.15625
- expand_bias: bfloat16 [3072], P('seq'), may hold values from -3 to 3
- contract_weight: bfloat16 [3072, 1536], P('seq'), may hold values from -0.109375 to 0.109375
- contract_bias: float32 [1536], replicated, may hold values from -3 to 3
- final_weight: bfloat16 [1536, 64], replicated, may hold values from -0.15625 to 0.15625
- final_bias: float32 [64], replicated, may hold values from -3 to 3
- latent: float32 [16, 512, 64], P('groups', 'seq'), parts along dimension 0, may hold values from -6 to 6
Outputs:
- velocity: float32 [16, 512, 64], P('groups', 'seq'), parts along dimension 0
- latent_next: float32 [16, 512, 64], P('groups', 'seq'), parts along dimension 0
There are 4 independent parts, one for each index of `groups`. A program takes and returns all parts, laid end to end along the dimension named above; an argument that names none is the same for every part. Nothing has to cross between parts.
Inputs may be any that keep to these rules, and one draw needn't show every extreme that they name: `slot_of`: each row number appears once.
All inputs are finite; a program needn't handle non-finite values.
Results may differ from a plain program's by a relative error of at most 0.0033.
The roundings to bfloat16 on the way count: a program that leaves them out, or rounds other values in their place, can miss the bound.
Values may be sent and summed in bfloat16 or wider, within the bound.
A program may use at most 128 MiB of HBM per device.

v0:
```python
import math

import jax
import jax.numpy as jnp
from jax import lax
from jax.sharding import PartitionSpec as P

HEADS = 24
HEAD_DIM = 64
PATCH = 64
NSTEPS = 28


guidance_scale = 7.0
rescale_mix = 0.7
time_shift = 3.0


def side_by_side(arrays, axis, split_dim, concat_dim, along):
    both = jnp.concatenate(arrays, axis=along)
    whole, at, done = (
        lax.all_to_all(both, axis, split_axis=split_dim, concat_axis=concat_dim, tiled=True),
        0,
        [],
    )
    for a in arrays:
        done.append(lax.slice_in_dim(whole, at, at + a.shape[along], axis=along))
        at += a.shape[along]
    return tuple(done)


def sent_together(arrays, axis, dim, along):
    columns = [a.reshape(*a.shape[:along], -1) for a in arrays]
    both = jnp.concatenate(columns, axis=along)
    whole, at, done = (lax.all_gather(both, axis, axis=dim, tiled=True), 0, [])
    for a, column in zip(arrays, columns):
        piece = whole[..., at : at + column.shape[along]]
        done.append(piece.reshape(*piece.shape[:along], *a.shape[along:]))
        at += column.shape[along]
    return tuple(done)


def sent_to_all(shard, axis):
    devices = lax.axis_size(axis)
    return lax.all_to_all(
        jnp.broadcast_to(shard[None], (devices, *shard.shape)), axis, 0, 0, tiled=True
    )


def taken_together(shard, axis):
    everything = sent_to_all(shard, axis)
    return jnp.sum(everything, axis=0)


def to_items(tensor):
    rows_batch, length, _ = tensor.shape
    return (
        tensor.reshape(rows_batch, length, HEADS, HEAD_DIM)
        .transpose(0, 2, 1, 3)
        .reshape(rows_batch * HEADS, length, HEAD_DIM)
    )


def attend_blocks(queries, keys_img, values_img, keys_txt, values_txt, length):
    total_rows = queries.shape[0]
    block_rows = 512
    keys_all = jnp.concatenate([keys_img, keys_txt], axis=0)
    values_all = jnp.concatenate([values_img, values_txt], axis=0)
    column = jnp.arange(keys_all.shape[0], dtype=jnp.int32)
    keep = column < keys_img.shape[0] + length

    def one_block(query_block):
        scores = jnp.dot(query_block, keys_all.T, preferred_element_type=jnp.float32) * (
            1.0 / math.sqrt(HEAD_DIM)
        )
        scores = jnp.where(keep[None, :], scores, -jnp.inf)
        top_score = jnp.max(scores, axis=1, keepdims=True)
        expon = jnp.exp(scores - top_score)
        weights = (expon / jnp.sum(expon, axis=1, keepdims=True)).astype(jnp.bfloat16)
        return jnp.dot(weights, values_all, preferred_element_type=jnp.float32).astype(jnp.bfloat16)

    blocks = queries.reshape(total_rows // block_rows, block_rows, HEAD_DIM)
    return lax.map(one_block, blocks).reshape(total_rows, HEAD_DIM)


def modulate(values, shift, scale):
    centred = values - jnp.mean(values, axis=2, keepdims=True)
    variance = jnp.mean(centred * centred, axis=2, keepdims=True)
    return (centred * lax.rsqrt(variance + 1e-06) * (1.0 + scale) + shift).astype(jnp.bfloat16)


def sigma_at(time_value):
    return time_shift * time_value / (1.0 + (time_shift - 1.0) * time_value)


def body(
    img_query,
    img_key,
    img_value,
    txt_key,
    txt_value,
    txt_len,
    slot_of,
    step_index,
    residual,
    modulation,
    out_weight,
    out_bias,
    expand_weight,
    expand_bias,
    contract_weight,
    contract_bias,
    final_weight,
    final_bias,
    latent,
):
    rows_batch, img_local, model_width = img_query.shape
    prompts = rows_batch // 2
    seq_devices = lax.axis_size("seq")
    per_device = rows_batch * HEADS // seq_devices
    my_index = lax.axis_index("seq")
    item_len = jnp.repeat(txt_len, HEADS)
    own_len = lax.dynamic_slice_in_dim(item_len, my_index * per_device, per_device)
    queries = to_items(img_query)
    keys_img = to_items(img_key)
    values_img = to_items(img_value)
    keys_txt = to_items(txt_key)
    values_txt = to_items(txt_value)
    got_q, got_k, got_v, got_tk, got_tv = (
        *side_by_side((queries, keys_img, values_img), "seq", 0, 1, 2),
        *side_by_side((keys_txt, values_txt), "seq", 0, 1, 2),
    )

    def one_item(inputs):
        return attend_blocks(*inputs)

    outputs = lax.map(one_item, (got_q, got_k, got_v, got_tk, got_tv, own_len))
    returned = lax.all_to_all(outputs, "seq", split_axis=1, concat_axis=0, tiled=True)
    attended = (
        returned.reshape(rows_batch, HEADS, img_local, HEAD_DIM)
        .transpose(0, 2, 1, 3)
        .reshape(rows_batch * img_local, model_width)
    )
    projected = (
        jnp.dot(attended, out_weight, preferred_element_type=jnp.float32).reshape(
            rows_batch, img_local, model_width
        )
        + out_bias
    )
    hidden = residual.astype(jnp.float32) + modulation[:, 0:1, :] * projected
    ff_rows = modulate(hidden, modulation[:, 1:2, :], modulation[:, 2:3, :]).reshape(
        rows_batch * img_local, model_width
    )
    weight_in, bias_in, weight_out = sent_together(
        (expand_weight, expand_bias, contract_weight), "seq", 0, 1
    )
    pre_act = lax.dot_general(
        ff_rows, weight_in, (((1,), (1,)), ((), ())), preferred_element_type=jnp.float32
    ) + bias_in.astype(jnp.float32)
    act = jax.nn.gelu(pre_act, approximate=True).astype(jnp.bfloat16)
    ff_sum = jnp.dot(act, weight_out, preferred_element_type=jnp.float32)
    ff_out = ff_sum.reshape(rows_batch, img_local, model_width) + contract_bias
    ff_hidden = hidden + modulation[:, 3:4, :] * ff_out
    normed = modulate(ff_hidden, modulation[:, 4:5, :], modulation[:, 5:6, :])
    pred = (
        jnp.dot(
            normed.reshape(rows_batch * img_local, model_width),
            final_weight,
            preferred_element_type=jnp.float32,
        ).reshape(rows_batch, img_local, PATCH)
        + final_bias
    )
    cond_pred = pred[slot_of[:prompts]]
    uncond_pred = pred[slot_of[prompts:]]
    guided = uncond_pred + guidance_scale * (cond_pred - uncond_pred)
    step_float = step_index[0].astype(jnp.float32)
    delta = sigma_at(1.0 - (step_float + 1.0) / NSTEPS) - sigma_at(1.0 - step_float / NSTEPS)
    plain_part = (1.0 - rescale_mix) * guided
    local_sums = jnp.stack(
        [
            jnp.sum(cond_pred, axis=(1, 2)),
            jnp.sum(cond_pred * cond_pred, axis=(1, 2)),
            jnp.sum(guided, axis=(1, 2)),
            jnp.sum(guided * guided, axis=(1, 2)),
        ]
    )
    totals = taken_together(local_sums, "seq")
    count = float(img_local * seq_devices * PATCH)
    std_cond = jnp.sqrt((totals[1] - totals[0] * totals[0] / count) / (count - 1.0) + 1e-06)
    std_guided = jnp.sqrt((totals[3] - totals[2] * totals[2] / count) / (count - 1.0) + 1e-06)
    ratio = std_cond / std_guided
    scaled_part = rescale_mix * ratio[:, None, None] * guided
    velocity = scaled_part + plain_part
    latent_next = latent + delta * velocity
    return (velocity, latent_next)


def solution(mesh):
    in_specs = (
        P("groups", "seq", None),
        P("groups", "seq", None),
        P("groups", "seq", None),
        P("groups", "seq", None),
        P("groups", "seq", None),
        P("groups"),
        P("groups"),
        P("groups"),
        P("groups", "seq", None),
        P("groups", None, None),
        P(),
        P(),
        P("seq", None),
        P("seq"),
        P("seq", None),
        P(),
        P(),
        P(),
        P("groups", "seq", None),
    )
    out_specs = (P("groups", "seq", None), P("groups", "seq", None))
    return jax.shard_map(body, mesh=mesh, in_specs=in_specs, out_specs=out_specs, check_vma=False)
```

profile of v0, /device:TPU:37, one launch (start us, length us, event | category | flops | bytes accessed | tf_op | source)
XLA Modules:
  0.0 339.0 jit_solution(11784718771021624386)
XLA Ops:
  7.2 0.1 all-gather.2.cloned.1.call-start
  7.3 0.8 copy.82
  8.1 1.9 concatenate.17
  9.9 0.1 all-gather.2.cloned.1.call-update
  10.0 1.1 reshape.169
  11.1 0.2 reshape.171
  11.3 0.1 pad_maximum_fusion.1
  11.5 0.8 copy.76
  12.3 34.5 %all-to-all-start.1 = ((bf16[192,4,128]{2,1,0:T(4,128)(2,1)}), bf16[192,4,128]{2,1,0:T(4,128)(2,1)S(1)}, u32[]{:S(2)}, u32[]{:S(2)}) async-start(bf16[192,4,128]{2,1,0:T(4,128)(2,1)} %copy.76), calls=%async_computation.1 | async-start | bytes 393216 | tf_op jit(solution)/shard_map/all_to_all | solution.py:22
  46.8 0.2 reshape.165
  47.0 0.1 copy.71
  47.1 0.2 reshape.167
  47.3 0.1 copy.72
  47.4 0.2 reshape.163
  47.7 0.1 copy.70
  47.7 1.3 pad_maximum_fusion
  49.0 36.0 %all-to-all-done.1 = bf16[192,4,128]{2,1,0:T(4,128)(2,1)S(1)} async-done(((bf16[192,4,128]{2,1,0:T(4,128)(2,1)}), bf16[192,4,128]{2,1,0:T(4,128)(2,1)S(1)}, u32[]{:S(2)}, u32[]{:S(2)}) %all-to-all-start.1) | async-done | bytes 196640 | tf_op jit(solution)/shard_map/all_to_all | solution.py:22
  85.0 6.2 %all-to-all-start = ((bf16[192,8,192]{2,1,0:T(8,128)(2,1)}), bf16[192,8,192]{2,1,0:T(8,128)(2,1)S(1)}, u32[]{:S(2)}, u32[]{:S(2)}) async-start(bf16[192,8,192]{2,1,0:T(8,128)(2,1)} %pad_maximum_fusion), calls=%async_computation | async-start | bytes 1572864 | tf_op jit(solution)/shard_map/all_to_all | solution.py:22
  91.3 0.1 broadcast_in_dim.57
  91.3 0.1 reshape.162
  91.4 0.1 dynamic_slice.27
  91.5 0.1 copy.77
  91.6 0.1 fusion.86
  91.7 95.9 %all-to-all-done = bf16[192,8,192]{2,1,0:T(8,128)(2,1)S(1)} async-done(((bf16[192,8,192]{2,1,0:T(8,128)(2,1)}), bf16[192,8,192]{2,1,0:T(8,128)(2,1)S(1)}, u32[]{:S(2)}, u32[]{:S(2)}) %all-to-all-start) | async-done | bytes 589856 | tf_op jit(solution)/shard_map/all_to_all | solution.py:22
  187.6 0.3 fusion.85
  187.9 8.4 %while.10 = (s32[]{:T(128)}, bf16[3,512,64]{1,2,0:T(8,128)(2,1)S(1)}, s32[3]{0:T(128)S(1)}, bf16[3,512,64]{2,1,0:T(8,128)(2,1)S(1)}, bf16[3,512,64]{2,1,0:T(8,12...) while((s32[]{:T(128)}, ...), condition=%wide.region_3.4_spmd, body=%wide.region_0.3_spmd.sunk | while | flops 104234752 | bytes 5713809 | solution.py:137
  188.0 0.6 dynamic_slice.45
  189.2 0.5 fusion.99
  189.7 0.4 fusion.100
  190.1 0.6 fusion.101
  190.8 0.6 dynamic_slice.45
  192.0 0.5 fusion.99
  192.5 0.4 fusion.100
  192.9 0.6 fusion.101
  193.6 0.6 dynamic_slice.45
  194.9 0.5 fusion.99
  195.3 0.4 fusion.100
  195.7 0.6 fusion.101
  196.4 0.3 copy.78
  196.7 1.1 reshape.221
  197.8 5.4 %all-to-all-start.2 = ((bf16[64,2,768]{2,1,0:T(2,128)(2,1)}), bf16[64,2,768]{2,1,0:T(2,128)(2,1)S(1)}, u32[]{:S(2)}, u32[]{:S(2)}) async-start(bf16[64,2,768]{2,1,0:T(2,128)(2,1)} %reshape.221), calls=%async_computation.2 | async-start | bytes 393216 | tf_op jit(solution)/shard_map/all_to_all | solution.py:138
  203.2 0.1 compare_select_fusion.1
  203.3 39.0 %all-to-all-done.2 = bf16[64,2,768]{2,1,0:T(2,128)(2,1)S(1)} async-done(((bf16[64,2,768]{2,1,0:T(2,128)(2,1)}), bf16[64,2,768]{2,1,0:T(2,128)(2,1)S(1)}, u32[]{:S(2)}, u32[]{:S(2)}) %all-to-all-start.2) | async-done | bytes 196640 | tf_op jit(solution)/shard_map/all_to_all | solution.py:138
  242.4 0.3 reshape.222
  242.7 0.1 copy.92
  242.8 0.1 copy.80
  242.8 0.1 copy.81
  242.9 0.3 dot_general.22
  243.2 0.4 copy-done.2
  243.6 3.4 %fusion.87 = (f32[8,8]{1,0:T(8,128)S(1)}, f32[8,8,1536]{2,1,0:T(8,128)S(1)}) fusion(f32[1536]{0:T(1024)S(1)} %copy-done.8, bf16[8,8,1536]{2,1,0:T(8,128)(2,1)S(1)} %dot_general.22, bf16[1536,1536]{1,0:T(8,128)(2,1)} %param.31, f32[8,1536]{1,0:T(8,128)S(1)} %get-tuple-element.98, bf16[8,8,1536]{2,1,0:T(8,128)(2,1)S(1)} %copy-done.2), kind=kOutput, calls=%fused_computation.102 | convolution fusion | flops 302481344 | bytes 5560576 | tf_op jit(solution)/shard_map/dot_general | solution.py:145
  247.0 0.2 multiply_reduce_fusion.1
  247.2 27.7 %all-gather.2.cloned.1.call-done = bf16[3072,3073]{1,0:T(8,128)(2,1)} async-done(((bf16[48,3073]{1,0:T(8,128)(2,1)}), bf16[3072,3073]{1,0:T(8,128)(2,1)}) %all-gather.2.cloned.1.call-update) | async-done | bytes 18880528 | tf_op jit(solution)/shard_map/all_gather | solution.py:35
  274.9 1.4 convert_reduce_fusion
  276.3 9.6 %fusion.88 = (f32[8,8]{1,0:T(8,128)S(1)}, f32[8,8,1536]{2,1,0:T(8,128)S(1)}) fusion(f32[8,8,1536]{2,1,0:T(8,128)S(1)} %get-tuple-element.105, f32[1536]{0:T(1024)S(1)} %copy-done.12, bf16[3072,3073]{1,0:T(8,128)(2,1)} %all-gather.2.cloned.1.call-done, f32[3072]{0:T(1024)S(1)} %convert_reduce_fusion, f32[8,1536]{1,0:T(8,128)S(1)} %get-tuple-element.95, ...), kind=kOutput, calls=%fused_computation.103 | convolution fusion | flops 1210810368 | bytes 20230400 | tf_op jit(solution)/shard_map/dot_general | solution.py:161
  285.9 0.2 multiply_reduce_fusion
  286.2 0.3 convolution_add_fusion
  286.4 0.6 gather_fusion
  287.0 0.6 gather_fusion.1
  287.5 0.1 fusion.83
  287.7 0.7 broadcast_in_dim.60
  288.3 13.0 %all-to-all-start.3 = ((f32[64,4,4]{2,1,0:T(4,128)}), f32[64,4,4]{2,1,0:T(4,128)S(1)}, u32[]{:S(2)}, u32[]{:S(2)}) async-start(f32[64,4,4]{2,1,0:T(4,128)} %broadcast_in_dim.60), calls=%async_computation.3 | async-start | bytes 262144 | tf_op jit(solution)/shard_map/all_to_all | solution.py:45
  302.1 29.3 %all-to-all-done.3 = f32[64,4,4]{2,1,0:T(4,128)S(1)} async-done(((f32[64,4,4]{2,1,0:T(4,128)}), f32[64,4,4]{2,1,0:T(4,128)S(1)}, u32[]{:S(2)}, u32[]{:S(2)}) %all-to-all-start.3) | async-done | bytes 4128 | tf_op jit(solution)/shard_map/all_to_all | solution.py:45
  331.4 0.1 reduce_sum.99
  331.5 0.7 multiply_add_fusion
  (46 shorter events, 0.4 us)
Async XLA Ops:
  7.2 279.0 %copy-start = (bf16[1536,64]{0,1:T(8,128)(2,1)S(1)}, bf16[1536,64]{0,1:T(8,128)(2,1)}, u32[]{:S(2)}) copy-start(bf16[1536,64]{0,1:T(8,128)(2,1)} %param.37) | copy-start | bytes 589828
  7.2 3.9 %copy-start.6 = (bf16[8,4,1536]{2,1,0:T(4,128)(2,1)S(1)}, bf16[8,4,1536]{2,1,0:T(4,128)(2,1)}, u32[]{:S(2)}) copy-start(bf16[8,4,1536]{2,1,0:T(4,128)(2,1)} %param.25) | copy-start | bytes 294916
  7.2 267.7 %all-gather.2.cloned.1.call-start = ((), (), s32[]{:S(2)}) async-start(), calls=%async_computation.4 | async-start | bytes 19968000 | tf_op jit(solution)/shard_map/all_gather | solution.py:35
  9.9 36.8 %copy-start.3 = (bf16[8,8,1536]{2,1,0:T(8,128)(2,1)S(1)}, bf16[8,8,1536]{2,1,0:T(8,128)(2,1)}, u32[]{:S(2)}) copy-start(bf16[8,8,1536]{2,1,0:T(8,128)(2,1)} %param.22) | copy-start | bytes 589828
  11.3 35.8 %copy-start.4 = (bf16[8,8,1536]{2,1,0:T(8,128)(2,1)S(1)}, bf16[8,8,1536]{2,1,0:T(8,128)(2,1)}, u32[]{:S(2)}) copy-start(bf16[8,8,1536]{2,1,0:T(8,128)(2,1)} %param.23) | copy-start | bytes 589828
  12.3 35.1 %copy-start.5 = (bf16[8,8,1536]{2,1,0:T(8,128)(2,1)S(1)}, bf16[8,8,1536]{2,1,0:T(8,128)(2,1)}, u32[]{:S(2)}) copy-start(bf16[8,8,1536]{2,1,0:T(8,128)(2,1)} %param.21) | copy-start | bytes 589828
  12.3 72.7 %all-to-all-start.1 = ((bf16[192,4,128]{2,1,0:T(4,128)(2,1)}), bf16[192,4,128]{2,1,0:T(4,128)(2,1)S(1)}, u32[]{:S(2)}, u32[]{:S(2)}) async-start(bf16[192,4,128]{2,1,0:T(4,128)(2,1)} %copy.76), calls=%async_computation.1 | async-start | bytes 393216 | tf_op jit(solution)/shard_map/all_to_all | solution.py:22
  47.7 43.5 %copy-start.11 = (s32[8]{0:T(128)S(1)}, s32[8]{0:T(128)}, u32[]{:S(2)}) copy-start(s32[8]{0:T(128)} %param.26) | copy-start | bytes 100
  85.0 102.5 %all-to-all-start = ((bf16[192,8,192]{2,1,0:T(8,128)(2,1)}), bf16[192,8,192]{2,1,0:T(8,128)(2,1)S(1)}, u32[]{:S(2)}, u32[]{:S(2)}) async-start(bf16[192,8,192]{2,1,0:T(8,128)(2,1)} %pad_maximum_fusion), calls=%async_computation | async-start | bytes 1572864 | tf_op jit(solution)/shard_map/all_to_all | solution.py:22
  196.3 6.9 %copy-start.9 = (s32[8]{0:T(128)S(1)}, s32[8]{0:T(128)}, u32[]{:S(2)}) copy-start(s32[8]{0:T(128)} %param.27) | copy-start | bytes 100
  196.4 6.9 %copy-start.1 = (f32[8,6,1536]{2,0,1:T(8,128)S(1)}, f32[8,6,1536]{2,0,1:T(8,128)}, u32[]{:S(2)}) copy-start(f32[8,6,1536]{2,0,1:T(8,128)} %param.30) | copy-start | bytes 884740
  197.8 44.6 %all-to-all-start.2 = ((bf16[64,2,768]{2,1,0:T(2,128)(2,1)}), bf16[64,2,768]{2,1,0:T(2,128)(2,1)S(1)}, u32[]{:S(2)}, u32[]{:S(2)}) async-start(bf16[64,2,768]{2,1,0:T(2,128)(2,1)} %reshape.221), calls=%async_computation.2 | async-start | bytes 393216 | tf_op jit(solution)/shard_map/all_to_all | solution.py:138
  242.7 0.9 copy-start.2
  242.7 0.9 copy-start.8
  243.6 32.7 %copy-start.12 = (f32[1536]{0:T(1024)S(1)}, f32[1536]{0:T(1024)}, u32[]{:S(2)}) copy-start(f32[1536]{0:T(1024)} %param.36) | copy-start | bytes 18436
  276.3 9.8 %copy-start.10 = (f32[64]{0:T(128)S(1)}, f32[64]{0:T(128)}, u32[]{:S(2)}) copy-start(f32[64]{0:T(128)} %param.38) | copy-start | bytes 772
  285.9 45.6 %copy-start.7 = (f32[4,8,64]{2,1,0:T(8,128)S(1)}, f32[4,8,64]{2,1,0:T(8,128)}, u32[]{:S(2)}) copy-start(f32[4,8,64]{2,1,0:T(8,128)} %param.39) | copy-start | bytes 24580
  288.3 43.1 %all-to-all-start.3 = ((f32[64,4,4]{2,1,0:T(4,128)}), f32[64,4,4]{2,1,0:T(4,128)S(1)}, u32[]{:S(2)}, u32[]{:S(2)}) async-start(f32[64,4,4]{2,1,0:T(4,128)} %broadcast_in_dim.60), calls=%async_computation.3 | async-start | bytes 262144 | tf_op jit(solution)/shard_map/all_to_all | solution.py:45
Sparse Core Ops, SparseCore 0:
  10.1 264.7 all-gather.1
where the time goes:
time: 340 us; the launch traced here: 339 us
  waiting for transfers between devices  228 us (67%)
  starting transfers between devices  59.2 us (17%)
  matrix products  16.5 us (5%)
  between operations  15.2 us (4%)
  local copies, waits for them, and re-layouts  12.7 us (4%)
  other arithmetic  5.44 us (2%)
    all_to_all x2, waiting for transfers between devices, side_by_side(): lax.all_to_all(both, axis, split_axis=split_dim, concat_axis=concat_dim,...  132 us
    all_to_all x2, starting transfers between devices, side_by_side(): lax.all_to_all(both, axis, split_axis=split_dim, concat_axis=concat_dim,...  40.6 us
    all_to_all x1, waiting for transfers between devices, body(): lax.all_to_all(outputs, 'seq', split_axis=1, concat_axis=0, tiled=True)  39 us
    all_to_all x1, waiting for transfers between devices, sent_to_all(): lax.all_to_all(jnp.broadcast_to(shard[None], (devices, *shard.shape)), ax...  29.3 us
    all_gather x1, waiting for transfers between devices, sent_together(): whole, at, done = (lax.all_gather(both, axis, axis=dim, tiled=True), 0, [])  27.7 us
    all_to_all x1, starting transfers between devices, sent_to_all(): lax.all_to_all(jnp.broadcast_to(shard[None], (devices, *shard.shape)), ax...  13 us
    dot_general x1, matrix products, body(): ff_sum = jnp.dot(act, weight_out, preferred_element_type=jnp.float32)  9.58 us
  transfers between devices with their start and end apart: 5, of which 5 were waited for; matrix products, arithmetic and copies ran while one was open for 5% of the time, Pallas kernels for 0%

commit v1 on v0

v1 whole, which is shorter than its diff:
```python
import functools
import math

import jax
import jax.numpy as jnp
from jax import lax
from jax.experimental import pallas as pl
from jax.experimental.pallas import tpu as pltpu
from jax.sharding import PartitionSpec as P

HEADS = 24
HEAD_DIM = 64
PATCH = 64
NSTEPS = 28
ITEMS = 3
LANES = 128
MESH = pl.DeviceIdType.MESH

guidance_scale = 7.0
rescale_mix = 0.7
time_shift = 3.0

SENDS_PER_STEP = 63
ATTEND_AT = 12
LAG = 2
CHUNK = 16

f32 = jnp.float32
bf16 = jnp.bfloat16


def sigma_at(time_value):
    return time_shift * time_value / (1.0 + (time_shift - 1.0) * time_value)


def roll(x, shift, axis):
    return pltpu.roll(x, shift, axis)


def modulate(values, shift, scale):
    centred = values - jnp.mean(values, axis=2, keepdims=True)
    variance = jnp.mean(centred * centred, axis=2, keepdims=True)
    return (centred * lax.rsqrt(variance + 1e-06) * (1.0 + scale) + shift)


def kernel(
    sizes,
    txt_len, slot_of, step_index,
    img_query, img_key, img_value, txt_key, txt_value,
    residual, modulation, out_weight, out_bias, expand_weight, expand_bias,
    contract_weight, contract_bias, final_weight, final_bias, latent,
    velocity_out, latent_out,
    wall, ow_v, pack, got, outb, back, attended, bias_all, bias_rows, bias_units, sums_all, hidden, ff_in, acc, pred_v, guided_v,
    in_sem, w_sem, qkv_send, qkv_recv, ret_send, ret_recv, own_recv, x_recv, y_recv, d_recv, sib_recv,
    ring_send, sib_send, x_send, y_send, xr_send, yr_send, bias_send, bias_recv, sums_send, sums_recv,
):
    groups, n, y_size, per_seq = sizes
    chips = n // 2
    half = chips // 2
    g = lax.axis_index("groups")
    me = lax.axis_index("seq")
    core = lax.rem(me, 2)
    sibling = me + 1 - 2 * core
    right = lax.rem(me + 2, n)
    left = lax.rem(me + n - 2, n)
    gy = lax.rem(g, 2)
    gx = lax.rem(g // y_size, 2)
    y_partner = g + 1 - 2 * gy
    x_partner = g + y_size * (1 - 2 * gx)
    q = 2 * gx + gy
    qx = 2 * (1 - gx) + gy
    qy = 2 * gx + 1 - gy
    qd = 3 - q
    width = wall.shape[-1]

    barrier = pltpu.get_barrier_semaphore()

    def greet(j, c):
        pl.semaphore_signal(barrier, inc=1, device_id=(g, lax.rem(me + j, n)), device_id_type=MESH)
        return c

    lax.fori_loop(1, n, greet, 0)
    pl.semaphore_signal(barrier, inc=1, device_id=(x_partner, me), device_id_type=MESH)
    pl.semaphore_signal(barrier, inc=1, device_id=(y_partner, me), device_id_type=MESH)

    own_copies = []
    for part in range(4):
        columns = pl.ds(part * width, width)
        own_copies.append(
            pltpu.make_async_copy(expand_weight.at[:, columns], wall.at[part, 0, me], w_sem.at[part, 0])
        )
        own_copies.append(
            pltpu.make_async_copy(contract_weight.at[:, columns], wall.at[part, 1, me], w_sem.at[part, 1])
        )
    for copy in own_copies:
        copy.start()
    ow_copy = pltpu.make_async_copy(out_weight, ow_v, in_sem.at[0])
    ow_copy.start()

    img_local = img_query.shape[1]
    batch = img_query.shape[0]
    lane = lax.broadcasted_iota(jnp.int32, (batch, 8, LANES), 2)
    sub = lax.broadcasted_iota(jnp.int32, (batch, 8, LANES), 1)
    low = sub < 4
    same = low == (lane < 64)

    def paired(x):
        return jnp.where(same, x, roll(roll(x, 64, 2), 4, 1))

    sub4 = lax.rem(sub, 4)
    for pair in range(HEADS // 2):
        cols = slice(pair * LANES, (pair + 1) * LANES)
        zq = paired(img_query[:, :, cols].astype(f32))
        zk = paired(img_key[:, :, cols].astype(f32))
        zv = paired(img_value[:, :, cols].astype(f32))
        tk = txt_key[:, :, cols].astype(f32)
        tv = txt_value[:, :, cols].astype(f32)
        t = jnp.concatenate([tk, tv], axis=1)
        swapped = roll(t, 64, 2)
        t_same = (sub4 < 2) == (lane < 64)
        zt = jnp.where(t_same, t, jnp.where(sub4 < 2, roll(swapped, 6, 1), roll(swapped, 2, 1)))
        t_even = jnp.where(sub < 6, roll(zt, 4, 1), roll(zt, 2, 1))
        t_odd = jnp.where(sub < 6, roll(zt, 2, 1), zt)
        for odd in range(2):
            head = 2 * pair + odd
            if odd == 0:
                top = jnp.where(low, zq, roll(zk, 4, 1))
                bottom = jnp.where(low, zv, t_even)
            else:
                top = jnp.where(low, roll(zq, 4, 1), zk)
                bottom = jnp.where(low, roll(zv, 4, 1), t_odd)
            block = jnp.concatenate([top, bottom], axis=1).astype(bf16)
            for b in range(batch):
                pack[head % ITEMS, per_seq * b + head // ITEMS] = block[b]

    my_b = me // per_seq
    my_k = lax.rem(me, per_seq)
    bias_all[me] = expand_bias[...]
    for i in range(ITEMS):
        got[i, me] = pack[i, me]

    for copy in own_copies:
        copy.wait()
    pl.semaphore_wait(barrier, n + 1)

    def drain(ref, sem):
        pltpu.make_async_copy(ref, ref, sem).wait()

    def offset(j):
        return jnp.where(lax.rem(j, 2) == 0, n // 2 + j // 2, n // 2 - j // 2)

    def ring(slot, direction, k, to):
        return pltpu.make_async_remote_copy(
            wall.at[q, :, slot], wall.at[q, :, slot], ring_send.at[direction], own_recv.at[direction, k],
            device_id=(g, to), device_id_type=MESH,
        )

    def to_sibling(part, slot):
        return pltpu.make_async_remote_copy(
            wall.at[part, :, slot], wall.at[part, :, slot], sib_send.at[part], sib_recv.at[part],
            device_id=(g, sibling), device_id_type=MESH,
        )

    def across(part, slot, send, recv, partner):
        return pltpu.make_async_remote_copy(
            wall.at[part, :, slot], wall.at[part, :, slot], send, recv,
            device_id=(partner, me), device_id_type=MESH,
        )

    def slot_at(direction, k):
        if direction == 0:
            return lax.rem(me + n - 2 * k, n)
        return lax.rem(me + 2 * k, n)

    ring(me, 0, 1, right).start()
    ring(me, 1, 1, left).start()
    for part in range(4):
        to_sibling(part, me).start()

    def send_bias(j, c):
        peer = lax.rem(me + offset(j), n)
        pltpu.make_async_remote_copy(
            bias_all.at[me], bias_all.at[me], bias_send, bias_recv,
            device_id=(g, peer), device_id_type=MESH,
        ).start()
        return c

    def send_item(index, c):
        i = index // (n - 1)
        peer = lax.rem(me + offset(lax.rem(index, n - 1) + 1), n)
        pltpu.make_async_remote_copy(
            pack.at[i, peer], got.at[i, me], qkv_send.at[i], qkv_recv.at[i],
            device_id=(g, peer), device_id_type=MESH,
        ).start()
        return c

    def attend(i):
        drain(got.at[i, pl.ds(0, n - 1)], qkv_recv.at[i])
        x = got[i].astype(f32)
        top = x[:, 0:8, :].reshape(n // 2, 2, 8, LANES)
        bottom = x[:, 8:16, :].reshape(n // 2, 2, 8, LANES)
        sub_ = lax.broadcasted_iota(jnp.int32, (n // 2, 8, LANES), 1)
        a, b = top[:, 0], top[:, 1]
        c, d = bottom[:, 0], bottom[:, 1]
        qs = jnp.where(sub_ < 4, a, roll(b, 4, 1)).reshape(4 * n, LANES)
        ks = jnp.where(sub_ < 4, roll(a, 4, 1), b).reshape(4 * n, LANES)
        vs = jnp.where(sub_ < 4, c, roll(d, 4, 1)).reshape(4 * n, LANES)
        t = jnp.where(sub_ < 4, roll(c, 4, 1), d).reshape(n // 4, 2, 8, LANES)
        t0, t1 = t[:, 0], t[:, 1]
        sub_t = lax.rem(lax.broadcasted_iota(jnp.int32, (n // 4, 8, LANES), 1), 4)
        tks = jnp.where(sub_t < 2, t0, roll(t1, 2, 1)).reshape(2 * n, LANES)
        tvs = jnp.where(sub_t < 2, roll(t0, 6, 1), t1).reshape(2 * n, LANES)
        kk = jnp.concatenate([ks, tks], axis=0)
        vv = jnp.concatenate([vs, tvs], axis=0)
        keys = jnp.concatenate([kk, roll(kk, 64, 1)], axis=0).astype(bf16)
        vals = jnp.concatenate([vv, roll(vv, 64, 1)], axis=0).astype(bf16)
        rows = 6 * n
        col = lax.broadcasted_iota(jnp.int32, (1, 2 * rows), 1)
        swap = (col >= rows).astype(jnp.int32)
        m = col - swap * rows - 4 * n
        s8 = m % 8
        source = 4 * (m // 8) + 2 * ((s8 % 4) // 2) + s8 // 4
        token = 4 * source + m % 2
        length = txt_len[my_b]
        lane_q = lax.broadcasted_iota(jnp.int32, (4 * n, LANES), 1)
        outs = []
        for side in range(2):
            inside = (lane_q < 64) if side == 0 else (lane_q >= 64)
            qa = jnp.where(inside, qs, 0.0).astype(bf16)
            scores = lax.dot_general(
                qa, keys, (((1,), (1,)), ((), ())), preferred_element_type=f32
            ) * (1.0 / math.sqrt(HEAD_DIM))
            which = swap if side == 0 else 1 - swap
            keep = (m < 0) | (token + 2 * which < length)
            scores = jnp.where(keep, scores, -jnp.inf)
            top_score = jnp.max(scores, axis=1, keepdims=True)
            expon = jnp.exp(scores - top_score)
            weights = (expon / jnp.sum(expon, axis=1, keepdims=True)).astype(bf16)
            outs.append(jnp.dot(weights, vals, preferred_element_type=f32))
        both = jnp.where(lane_q < 64, outs[0], outs[1]).reshape(n // 2, 8, LANES).astype(bf16)
        outb[i] = jnp.stack([both[:, 0:4], both[:, 4:8]], axis=1).reshape(n, 4, LANES)

        def send_back(j, carry):
            peer = lax.rem(me + offset(j), n)
            pltpu.make_async_remote_copy(
                outb.at[i, peer], back.at[i, me], ret_send.at[i], ret_recv.at[i],
                device_id=(g, peer), device_id_type=MESH,
            ).start()
            return carry

        lax.fori_loop(1, n, send_back, 0)
        back[i, me] = outb[i, me]

    def step(k, carry):
        total = ITEMS * (n - 1)
        first = (k - 1) * SENDS_PER_STEP

        @pl.when(first < total)
        def _():
            lax.fori_loop(0, SENDS_PER_STEP, lambda s, c: send_item(first + s, c), 0)

        @pl.when(k == 4)
        def _():
            lax.fori_loop(1, n, send_bias, 0)

        for direction, last, onward in ((0, half, right), (1, half - 1, left)):

            @pl.when(k <= last)
            def _():
                slot = slot_at(direction, k)
                ring(slot, direction, k, onward).wait_recv()

                @pl.when(k < last)
                def _():
                    ring(slot, direction, k + 1, onward).start()

                across(q, slot, x_send, x_recv.at[direction, k], x_partner).start()
                across(q, slot, y_send, y_recv.at[direction, k], y_partner).start()
                to_sibling(q, slot).start()

        for direction, last in ((0, half), (1, half - 1)):
            late = k - LAG

            @pl.when((late >= 1) & (late <= last))
            def _():
                slot = slot_at(direction, late)
                across(qx, slot, x_send, x_recv.at[direction, late], x_partner).wait_recv()
                if direction == 0:
                    across(qx, slot, yr_send, d_recv.at[direction, late], y_partner).start()
                to_sibling(qx, slot).start()
                across(qy, slot, y_send, y_recv.at[direction, late], y_partner).wait_recv()
                if direction == 1:
                    across(qy, slot, xr_send, d_recv.at[direction, late], x_partner).start()
                to_sibling(qy, slot).start()

            later = k - 2 * LAG

            @pl.when((later >= 1) & (later <= last))
            def _():
                slot = slot_at(direction, later)
                across(qd, slot, xr_send, d_recv.at[direction, later], x_partner).wait_recv()
                to_sibling(qd, slot).start()

        at = k - ATTEND_AT

        @pl.when((at >= 0) & (lax.rem(at, 2) == 0) & (at // 2 < ITEMS))
        def _():
            attend(at // 2)

        return carry

    lax.fori_loop(1, half + 2 * LAG + 1, step, 0)

    chunks = len(range(0, n, CHUNK))
    hidden_own = wall.shape[3]
    chunk_units = CHUNK * hidden_own
    drain(bias_all.at[pl.ds(0, n - 1)], bias_recv)
    for r in range(n):
        bias_rows[r : r + 1, :] = bias_all[r]
    unit = lax.broadcasted_iota(jnp.int32, (LANES, chunk_units), 1)
    block_of = ((unit.astype(f32) + 0.5) * (1.0 / hidden_own)).astype(jnp.int32)
    pick = jnp.where(
        unit - block_of * hidden_own == lax.broadcasted_iota(jnp.int32, (LANES, chunk_units), 0), 1.0, 0.0
    ).astype(bf16)
    mine = block_of[:CHUNK] == lax.broadcasted_iota(jnp.int32, (CHUNK, chunk_units), 0)
    for c in range(chunks):
        spread = jnp.dot(
            bias_rows[c * CHUNK : (c + 1) * CHUNK, :].astype(bf16), pick, preferred_element_type=f32
        )
        bias_units[c] = jnp.sum(jnp.where(mine, spread, 0.0), axis=0, keepdims=True)

    for i in range(ITEMS):
        drain(back.at[i, pl.ds(0, n - 1)], ret_recv.at[i])
    for pair in range(HEADS // 2):
        cols = slice(pair * LANES, (pair + 1) * LANES)
        halves = []
        for head in (2 * pair, 2 * pair + 1):
            i, k = head % ITEMS, head // ITEMS
            halves.append(jnp.stack([back[i, per_seq * b + k].astype(f32) for b in range(batch)], axis=0))
        z = jnp.concatenate(halves, axis=1)
        attended[:, cols] = paired(z).reshape(batch * img_local, LANES).astype(bf16)

    ow_copy.wait()
    d_model = attended.shape[-1]
    shape3 = (batch, img_local, d_model)
    projected = jnp.dot(attended[...], ow_v[...], preferred_element_type=f32).reshape(shape3) + out_bias[...]
    hidden[...] = residual[...].astype(f32) + modulation[:, 0:1, :] * projected
    ff_in[...] = (
        modulate(hidden[...], modulation[:, 1:2, :], modulation[:, 2:3, :])
        .reshape(batch * img_local, d_model)
        .astype(bf16)
    )
    acc[...] = jnp.zeros_like(acc)

    for part in range(4):
        drain(wall.at[part, :, pl.ds(0, chips)], sib_recv.at[part])

    def feed(c, carry):
        blocks = pl.ds(c * CHUNK, CHUNK)
        pre = bias_units[c]
        for part in range(4):
            w = wall[part, 0, blocks].reshape(chunk_units, width)
            pre = pre + lax.dot_general(
                ff_in[:, part * width : (part + 1) * width], w,
                (((1,), (1,)), ((), ())), preferred_element_type=f32,
            )
        act = (0.5 * pre * (1.0 + jnp.tanh(math.sqrt(2.0 / math.pi) * (pre + 0.044715 * pre * pre * pre)))).astype(bf16)
        for part in range(4):
            w = wall[part, 1, blocks].reshape(chunk_units, width)
            acc[:, part * width : (part + 1) * width] += jnp.dot(act, w, preferred_element_type=f32)
        return carry

    lax.fori_loop(0, chunks, feed, 0)

    ff_hidden = hidden[...] + modulation[:, 3:4, :] * (acc[...].reshape(shape3) + contract_bias[...])
    normed = (
        modulate(ff_hidden, modulation[:, 4:5, :], modulation[:, 5:6, :])
        .reshape(batch * img_local, d_model)
        .astype(bf16)
    )
    pred = jnp.dot(normed, final_weight[...], preferred_element_type=f32) + final_bias[...]
    pred_v[...] = pred.reshape(batch, img_local, PATCH)
    prompts = batch // 2
    lane_row = lax.broadcasted_iota(jnp.int32, (1, LANES), 1)
    row = jnp.zeros((1, LANES), f32)

    def full_sum(x):
        return jnp.sum(jnp.sum(x, axis=1, keepdims=True), axis=0, keepdims=True)

    for p in range(prompts):
        cond = pred_v[slot_of[p]]
        uncond = pred_v[slot_of[prompts + p]]
        guided = uncond + guidance_scale * (cond - uncond)
        guided_v[p] = guided
        for s, value in enumerate((cond, cond * cond, guided, guided * guided)):
            row = jnp.where(lane_row == s * prompts + p, full_sum(value), row)
    sums_all[me] = row

    def send_sums(j, c):
        peer = lax.rem(me + offset(j), n)
        pltpu.make_async_remote_copy(
            sums_all.at[me], sums_all.at[me], sums_send, sums_recv,
            device_id=(g, peer), device_id_type=MESH,
        ).start()
        return c

    lax.fori_loop(1, n, send_sums, 0)

    for direction, count in ((0, half), (1, half - 1)):
        drain(wall.at[0, :, pl.ds(0, count)], ring_send.at[direction])
    for part in range(4):
        drain(wall.at[part, :, pl.ds(0, chips)], sib_send.at[part])
    drain(wall.at[0, :, pl.ds(0, chips - 1)], x_send)
    drain(wall.at[0, :, pl.ds(0, chips - 1)], y_send)
    drain(wall.at[0, :, pl.ds(0, half - 1)], xr_send)
    drain(wall.at[0, :, pl.ds(0, half)], yr_send)
    drain(bias_all.at[pl.ds(0, n - 1)], bias_send)
    for i in range(ITEMS):
        drain(pack.at[i, pl.ds(0, n - 1)], qkv_send.at[i])
        drain(outb.at[i, pl.ds(0, n - 1)], ret_send.at[i])
    drain(sums_all.at[pl.ds(0, n - 1)], sums_recv)
    drain(sums_all.at[pl.ds(0, n - 1)], sums_send)

    totals = jnp.sum(sums_all[...], axis=0)
    count = float(img_local * n * PATCH)
    step_float = jnp.full((img_local, PATCH), step_index[0], jnp.int32).astype(f32)
    delta = sigma_at(1.0 - (step_float + 1.0) / NSTEPS) - sigma_at(1.0 - step_float / NSTEPS)
    for p in range(prompts):
        t = [totals[:, s * prompts + p : s * prompts + p + 1] for s in range(4)]
        std_cond = jnp.sqrt((t[1] - t[0] * t[0] / count) / (count - 1.0) + 1e-06)
        std_guided = jnp.sqrt((t[3] - t[2] * t[2] / count) / (count - 1.0) + 1e-06)
        ratio = std_cond / std_guided
        guided = guided_v[p]
        velocity = rescale_mix * ratio * guided + (1.0 - rescale_mix) * guided
        velocity_out[p] = velocity
        latent_out[p] = latent[p] + delta * velocity


def body(
    y_size,
    groups,
    n,
    img_query,
    img_key,
    img_value,
    txt_key,
    txt_value,
    txt_len,
    slot_of,
    step_index,
    residual,
    modulation,
    out_weight,
    out_bias,
    expand_weight,
    expand_bias,
    contract_weight,
    contract_bias,
    final_weight,
    final_bias,
    latent,
):
    batch, img_local, d_model = img_query.shape
    prompts = batch // 2
    hidden_own = expand_weight.shape[0]
    per_seq = n // batch
    rows = batch * img_local
    bias_row = jnp.pad(expand_bias.astype(f32), (0, LANES - hidden_own)).reshape(1, LANES)
    vmem = pl.BlockSpec(memory_space=pltpu.VMEM)
    smem = pl.BlockSpec(memory_space=pltpu.SMEM)
    hbm = pl.BlockSpec(memory_space=pl.ANY)
    dma = pltpu.SemaphoreType.DMA
    half = n // 4
    return pl.pallas_call(
        functools.partial(kernel, (groups, n, y_size, per_seq)),
        out_shape=(jax.ShapeDtypeStruct(latent.shape, f32), jax.ShapeDtypeStruct(latent.shape, f32)),
        in_specs=[smem] * 3 + [vmem] * 7 + [hbm, vmem, hbm, vmem, hbm] + [vmem] * 4,
        out_specs=(vmem, vmem),
        scratch_shapes=[
            pltpu.VMEM((4, 2, n, hidden_own, d_model // 4), bf16),
            pltpu.VMEM((d_model, d_model), bf16),
            pltpu.VMEM((ITEMS, n, 16, LANES), bf16),
            pltpu.VMEM((ITEMS, n, 16, LANES), bf16),
            pltpu.VMEM((ITEMS, n, 4, LANES), bf16),
            pltpu.VMEM((ITEMS, n, 4, LANES), bf16),
            pltpu.VMEM((rows, d_model), bf16),
            pltpu.VMEM((n, 1, LANES), f32),
            pltpu.VMEM((n, LANES), f32),
            pltpu.VMEM((n // CHUNK, 1, CHUNK * hidden_own), f32),
            pltpu.VMEM((n, 1, LANES), f32),
            pltpu.VMEM((batch, img_local, d_model), f32),
            pltpu.VMEM((rows, d_model), bf16),
            pltpu.VMEM((rows, d_model), f32),
            pltpu.VMEM((batch, img_local, PATCH), f32),
            pltpu.VMEM((prompts, img_local, PATCH), f32),
            dma((1,)),
            dma((4, 2)),
            dma((ITEMS,)),
            dma((ITEMS,)),
            dma((ITEMS,)),
            dma((ITEMS,)),
            dma((2, half + 1)),
            dma((2, half + 1)),
            dma((2, half + 1)),
            dma((2, half + 1)),
            dma((4,)),
            dma((2,)),
            dma((4,)),
            dma,
            dma,
            dma,
            dma,
            dma,
            dma,
            dma,
            dma,
        ],
        compiler_params=pltpu.CompilerParams(
            collective_id=0, has_side_effects=True, vmem_limit_bytes=60 * 1024 * 1024
        ),
    )(
        txt_len, slot_of, step_index,
        img_query, img_key, img_value, txt_key, txt_value,
        residual, modulation, out_weight, out_bias.reshape(1, -1), expand_weight, bias_row,
        contract_weight, contract_bias.reshape(1, -1), final_weight, final_bias.reshape(1, -1), latent,
    )


def solution(mesh):
    in_specs = (
        P("groups", "seq", None),
        P("groups", "seq", None),
        P("groups", "seq", None),
        P("groups", "seq", None),
        P("groups", "seq", None),
        P("groups"),
        P("groups"),
        P("groups"),
        P("groups", "seq", None),
        P("groups", None, None),
        P(),
        P(),
        P("seq", None),
        P("seq"),
        P("seq", None),
        P(),
        P(),
        P(),
        P("groups", "seq", None),
    )
    out_specs = (P("groups", "seq", None), P("groups", "seq", None))
    groups, n = mesh.shape["groups"], mesh.shape["seq"]
    bits = groups.bit_length() - 1
    y_size = 1 << (bits - bits // 2)
    return jax.shard_map(
        functools.partial(body, y_size, groups, n),
        mesh=mesh, in_specs=in_specs, out_specs=out_specs, check_vma=False,
    )
```

time: 340 us -> 215 us (0.63)
  waiting for transfers between devices: 228 us -> 0 us
  Pallas kernels: 0 us -> 203 us
  starting transfers between devices: 59.2 us -> 0 us
  matrix products: 16.5 us -> 0 us
  between operations: 15.2 us -> 1.29 us
  other arithmetic: 5.44 us -> 1.23 us
  local copies, waits for them, and re-layouts: 12.7 us -> 8.96 us
    pallas_call x0 -> x1, Pallas kernels: none -> 203 us  [body(): pl.pallas_call(functools.partial(kernel, (groups, n, y_size, per_seq)), o...]
    all_to_all x4 -> x0, waiting for transfers between devices: 200 us -> none  [the longest x2 132 us: side_by_side(): lax.all_to_all(both, axis, split_axis=split_dim, concat_axis=concat_dim,...]
    all_to_all x4 -> x0, starting transfers between devices: 59.1 us -> none  [the longest x2 40.6 us: side_by_side(): lax.all_to_all(both, axis, split_axis=split_dim, concat_axis=concat_dim,...]
    all_gather x1 -> x0, waiting for transfers between devices: 27.7 us -> none  [sent_together(): whole, at, done = (lax.all_gather(both, axis, axis=dim, tiled=True), 0, [])]
    dot_general x9 -> x0, matrix products: 16.5 us -> none  [the longest x1 9.58 us: body(): ff_sum = jnp.dot(act, weight_out, preferred_element_type=jnp.float32)]
    unnamed x28 -> x4, local copies, waits for them, and re-layouts: 1.88 us -> 6.37 us
  transfers between devices with their start and end apart: 5 -> 0, of which waited for: 5 -> 0; matrix products, arithmetic and copies ran while one was open for 5% -> 0% of each run, Pallas kernels for 0% -> 0%
where the time goes in v1:
time: 215 us
  Pallas kernels  203 us (94%)
  local copies, waits for them, and re-layouts  8.96 us (4%)
    pallas_call x1, Pallas kernels, body(): pl.pallas_call(functools.partial(kernel, (groups, n, y_size, per_seq)), o...  203 us
    unnamed x4, local copies, waits for them, and re-layouts  6.37 us

profile of v1, /device:TPU:37, one launch (start us, length us, event | category | flops | bytes accessed | tf_op | source)
XLA Modules:
  0.0 214.9 jit_solution(17363544665252439288)
XLA Ops:
  1.3 1.2 bitcast_convert_fusion.expand_bias
  2.5 1.3 reshape.18.out_bias
  3.8 1.3 reshape.21.contract_bias
  5.1 1.9 copy.21.modulation
  7.0 1.9 copy.22.final_weight
  8.8 203.5 %shard_map.194 = (f32[4,8,64]{2,1,0:T(8,128)}, f32[4,8,64]{2,1,0:T(8,128)}) custom-call(s32[8]{0:T(128)} %txt_len.1, s32[8]{0:T(128)} %slot_of.1, s32[1]{0:T(128)S(6)} %copy.25.step_index, bf16[8,8,1536]{2,1,0:T(8,128)(2,1)} %img_query.1, bf16[8,8,1536]{2,1,0:T(8,128)(2,1)} %img_key.1, bf16[8,8,1536]{2,1,0:T(8,128)(2,1)} %img_value.1, ...), custom_call_target="tpu_custom_call" | custom-call | tf_op jit(solution)/shard_map/pallas_call | solution.py:474
  212.3 1.3 copy.26
  213.6 1.3 copy.27

commit v2 on v1

--- a/solution.py
+++ b/solution.py
@@ -20,9 +20,9 @@
 rescale_mix = 0.7
 time_shift = 3.0
 
-SENDS_PER_STEP = 63
-ATTEND_AT = 12
-LAG = 2
+SENDS_PER_STEP = 13
+ATTEND_AT = (7, 12, 17)
+LAG = 3
 CHUNK = 16
 
 f32 = jnp.float32
@@ -45,16 +45,17 @@
 
 def kernel(
     sizes,
-    txt_len, slot_of, step_index,
-    img_query, img_key, img_value, txt_key, txt_value,
-    residual, modulation, out_weight, out_bias, expand_weight, expand_bias,
-    contract_weight, contract_bias, final_weight, final_bias, latent,
-    velocity_out, latent_out,
-    wall, ow_v, pack, got, outb, back, attended, bias_all, bias_rows, bias_units, sums_all, hidden, ff_in, acc, pred_v, guided_v,
+    expand_weight, contract_weight, arrays, results, held,
+    wall, pack, got, outb, back, attended, bias_all, bias_rows, bias_units, sums_all, hidden, ff_in, acc, pred_v, guided_v,
     in_sem, w_sem, qkv_send, qkv_recv, ret_send, ret_recv, own_recv, x_recv, y_recv, d_recv, sib_recv,
     ring_send, sib_send, x_send, y_send, xr_send, yr_send, bias_send, bias_recv, sums_send, sums_recv,
 ):
     groups, n, y_size, per_seq = sizes
+    (
+        img_query, img_key, img_value, txt_key, txt_value, expand_bias, txt_len,
+        slot_of, step_index, residual, modulation, ow_v, out_bias, contract_bias, final_weight, final_bias, latent,
+    ) = held
+    early = 7
     chips = n // 2
     half = chips // 2
     g = lax.axis_index("groups")
@@ -83,6 +84,9 @@
     pl.semaphore_signal(barrier, inc=1, device_id=(x_partner, me), device_id_type=MESH)
     pl.semaphore_signal(barrier, inc=1, device_id=(y_partner, me), device_id_type=MESH)
 
+    in_copies = [pltpu.make_async_copy(a, h, in_sem.at[i]) for i, (a, h) in enumerate(zip(arrays, held))]
+    for copy in in_copies:
+        copy.start()
     own_copies = []
     for part in range(4):
         columns = pl.ds(part * width, width)
@@ -94,8 +98,8 @@
         )
     for copy in own_copies:
         copy.start()
-    ow_copy = pltpu.make_async_copy(out_weight, ow_v, in_sem.at[0])
-    ow_copy.start()
+    for copy in in_copies[:early]:
+        copy.wait()
 
     img_local = img_query.shape[1]
     batch = img_query.shape[0]
@@ -135,16 +139,20 @@
 
     my_b = me // per_seq
     my_k = lax.rem(me, per_seq)
-    bias_all[me] = expand_bias[...]
+    bias_all[me] = jnp.zeros((1, LANES), f32)
+    bias_all[me, 0:1, 0 : expand_bias.shape[0]] = expand_bias[...].astype(f32).reshape(1, -1)
     for i in range(ITEMS):
         got[i, me] = pack[i, me]
 
     for copy in own_copies:
         copy.wait()
-    pl.semaphore_wait(barrier, n + 1)
+    with jax.named_scope("barrier"):
+        pl.semaphore_wait(barrier, n + 1)
 
     def drain(ref, sem):
         pltpu.make_async_copy(ref, ref, sem).wait()
+
+    scope = jax.named_scope
 
     def offset(j):
         return jnp.where(lax.rem(j, 2) == 0, n // 2 + j // 2, n // 2 - j // 2)
@@ -195,7 +203,8 @@
         return c
 
     def attend(i):
-        drain(got.at[i, pl.ds(0, n - 1)], qkv_recv.at[i])
+        with scope("items"):
+            drain(got.at[i, pl.ds(0, n - 1)], qkv_recv.at[i])
         x = got[i].astype(f32)
         top = x[:, 0:8, :].reshape(n // 2, 2, 8, LANES)
         bottom = x[:, 8:16, :].reshape(n // 2, 2, 8, LANES)
@@ -214,28 +223,28 @@
         vv = jnp.concatenate([vs, tvs], axis=0)
         keys = jnp.concatenate([kk, roll(kk, 64, 1)], axis=0).astype(bf16)
         vals = jnp.concatenate([vv, roll(vv, 64, 1)], axis=0).astype(bf16)
-        rows = 6 * n
-        col = lax.broadcasted_iota(jnp.int32, (1, 2 * rows), 1)
-        swap = (col >= rows).astype(jnp.int32)
-        m = col - swap * rows - 4 * n
+        img, rows = 4 * n, 6 * n
+        m = lax.broadcasted_iota(jnp.int32, (1, 2 * n), 1)
         s8 = m % 8
-        source = 4 * (m // 8) + 2 * ((s8 % 4) // 2) + s8 // 4
-        token = 4 * source + m % 2
+        token = 4 * (4 * (m // 8) + 2 * ((s8 % 4) // 2) + s8 // 4) + m % 2
         length = txt_len[my_b]
         lane_q = lax.broadcasted_iota(jnp.int32, (4 * n, LANES), 1)
+        scale = 1.0 / math.sqrt(HEAD_DIM)
         outs = []
         for side in range(2):
             inside = (lane_q < 64) if side == 0 else (lane_q >= 64)
-            qa = jnp.where(inside, qs, 0.0).astype(bf16)
-            scores = lax.dot_general(
-                qa, keys, (((1,), (1,)), ((), ())), preferred_element_type=f32
-            ) * (1.0 / math.sqrt(HEAD_DIM))
-            which = swap if side == 0 else 1 - swap
-            keep = (m < 0) | (token + 2 * which < length)
-            scores = jnp.where(keep, scores, -jnp.inf)
+            qa = jnp.where(inside, qs * scale, 0.0).astype(bf16)
+            scores = lax.dot_general(qa, keys, (((1,), (1,)), ((), ())), preferred_element_type=f32)
+            pieces = []
+            for swap in range(2):
+                which = swap if side == 0 else 1 - swap
+                pieces.append(scores[:, swap * rows : swap * rows + img])
+                text = scores[:, swap * rows + img : (swap + 1) * rows]
+                pieces.append(jnp.where(token + 2 * which < length, text, -jnp.inf))
+            scores = jnp.concatenate(pieces, axis=1)
             top_score = jnp.max(scores, axis=1, keepdims=True)
             expon = jnp.exp(scores - top_score)
-            weights = (expon / jnp.sum(expon, axis=1, keepdims=True)).astype(bf16)
+            weights = (expon * (1.0 / jnp.sum(expon, axis=1, keepdims=True))).astype(bf16)
             outs.append(jnp.dot(weights, vals, preferred_element_type=f32))
         both = jnp.where(lane_q < 64, outs[0], outs[1]).reshape(n // 2, 8, LANES).astype(bf16)
         outb[i] = jnp.stack([both[:, 0:4], both[:, 4:8]], axis=1).reshape(n, 4, LANES)
@@ -257,7 +266,8 @@
 
         @pl.when(first < total)
         def _():
-            lax.fori_loop(0, SENDS_PER_STEP, lambda s, c: send_item(first + s, c), 0)
+            with scope("send"):
+                lax.fori_loop(first, jnp.minimum(first + SENDS_PER_STEP, total), send_item, 0)
 
         @pl.when(k == 4)
         def _():
@@ -268,7 +278,8 @@
             @pl.when(k <= last)
             def _():
                 slot = slot_at(direction, k)
-                ring(slot, direction, k, onward).wait_recv()
+                with scope("own"):
+                    ring(slot, direction, k, onward).wait_recv()
 
                 @pl.when(k < last)
                 def _():
@@ -284,11 +295,13 @@
             @pl.when((late >= 1) & (late <= last))
             def _():
                 slot = slot_at(direction, late)
-                across(qx, slot, x_send, x_recv.at[direction, late], x_partner).wait_recv()
+                with scope("x"):
+                    across(qx, slot, x_send, x_recv.at[direction, late], x_partner).wait_recv()
                 if direction == 0:
                     across(qx, slot, yr_send, d_recv.at[direction, late], y_partner).start()
                 to_sibling(qx, slot).start()
-                across(qy, slot, y_send, y_recv.at[direction, late], y_partner).wait_recv()
+                with scope("y"):
+                    across(qy, slot, y_send, y_recv.at[direction, late], y_partner).wait_recv()
                 if direction == 1:
                     across(qy, slot, xr_send, d_recv.at[direction, late], x_partner).start()
                 to_sibling(qy, slot).start()
@@ -298,14 +311,16 @@
             @pl.when((later >= 1) & (later <= last))
             def _():
                 slot = slot_at(direction, later)
-                across(qd, slot, xr_send, d_recv.at[direction, later], x_partner).wait_recv()
+                with scope("d"):
+                    across(qd, slot, xr_send, d_recv.at[direction, later], x_partner).wait_recv()
                 to_sibling(qd, slot).start()
 
-        at = k - ATTEND_AT
-
-        @pl.when((at >= 0) & (lax.rem(at, 2) == 0) & (at // 2 < ITEMS))
+        first_at, second_at, third_at = ATTEND_AT
+
+        @pl.when((k == first_at) | (k == second_at) | (k == third_at))
         def _():
-            attend(at // 2)
+            with scope("attend"):
+                attend((k >= second_at).astype(jnp.int32) + (k >= third_at).astype(jnp.int32))
 
         return carry
 
@@ -330,7 +345,8 @@
         bias_units[c] = jnp.sum(jnp.where(mine, spread, 0.0), axis=0, keepdims=True)
 
     for i in range(ITEMS):
-        drain(back.at[i, pl.ds(0, n - 1)], ret_recv.at[i])
+        with scope("ret"):
+            drain(back.at[i, pl.ds(0, n - 1)], ret_recv.at[i])
     for pair in range(HEADS // 2):
         cols = slice(pair * LANES, (pair + 1) * LANES)
         halves = []
@@ -340,20 +356,22 @@
         z = jnp.concatenate(halves, axis=1)
         attended[:, cols] = paired(z).reshape(batch * img_local, LANES).astype(bf16)
 
-    ow_copy.wait()
+    for copy in in_copies[early:]:
+        copy.wait()
     d_model = attended.shape[-1]
     shape3 = (batch, img_local, d_model)
-    projected = jnp.dot(attended[...], ow_v[...], preferred_element_type=f32).reshape(shape3) + out_bias[...]
-    hidden[...] = residual[...].astype(f32) + modulation[:, 0:1, :] * projected
+    projected = jnp.dot(attended[...], ow_v[...], preferred_element_type=f32).reshape(shape3) + out_bias[...].reshape(1, 1, -1)
+    hidden[...] = residual[...].astype(f32) + modulation[0][:, None, :] * projected
     ff_in[...] = (
-        modulate(hidden[...], modulation[:, 1:2, :], modulation[:, 2:3, :])
+        modulate(hidden[...], modulation[1][:, None, :], modulation[2][:, None, :])
         .reshape(batch * img_local, d_model)
         .astype(bf16)
     )
     acc[...] = jnp.zeros_like(acc)
 
     for part in range(4):
-        drain(wall.at[part, :, pl.ds(0, chips)], sib_recv.at[part])
+        with scope("sib"):
+            drain(wall.at[part, :, pl.ds(0, chips)], sib_recv.at[part])
 
     def feed(c, carry):
         blocks = pl.ds(c * CHUNK, CHUNK)
@@ -370,15 +388,18 @@
             acc[:, part * width : (part + 1) * width] += jnp.dot(act, w, preferred_element_type=f32)
         return carry
 
-    lax.fori_loop(0, chunks, feed, 0)
-
-    ff_hidden = hidden[...] + modulation[:, 3:4, :] * (acc[...].reshape(shape3) + contract_bias[...])
+    with scope("ffn"):
+        lax.fori_loop(0, chunks, feed, 0)
+
+    ff_hidden = hidden[...] + modulation[3][:, None, :] * (acc[...].reshape(shape3) + contract_bias[...].reshape(1, 1, -1))
     normed = (
-        modulate(ff_hidden, modulation[:, 4:5, :], modulation[:, 5:6, :])
+        modulate(ff_hidden, modulation[4][:, None, :], modulation[5][:, None, :])
         .reshape(batch * img_local, d_model)
         .astype(bf16)
     )
-    pred = jnp.dot(normed, final_weight[...], preferred_element_type=f32) + final_bias[...]
+    pred = lax.dot_general(
+        normed, final_weight[...], (((1,), (1,)), ((), ())), preferred_element_type=f32
+    ) + final_bias[...].reshape(1, -1)
     pred_v[...] = pred.reshape(batch, img_local, PATCH)
     prompts = batch // 2
     lane_row = lax.broadcasted_iota(jnp.int32, (1, LANES), 1)
@@ -406,6 +427,8 @@
 
     lax.fori_loop(1, n, send_sums, 0)
 
+    with scope("left"):
+        pass
     for direction, count in ((0, half), (1, half - 1)):
         drain(wall.at[0, :, pl.ds(0, count)], ring_send.at[direction])
     for part in range(4):
@@ -418,7 +441,8 @@
     for i in range(ITEMS):
         drain(pack.at[i, pl.ds(0, n - 1)], qkv_send.at[i])
         drain(outb.at[i, pl.ds(0, n - 1)], ret_send.at[i])
-    drain(sums_all.at[pl.ds(0, n - 1)], sums_recv)
+    with scope("sums"):
+        drain(sums_all.at[pl.ds(0, n - 1)], sums_recv)
     drain(sums_all.at[pl.ds(0, n - 1)], sums_send)
 
     totals = jnp.sum(sums_all[...], axis=0)
@@ -432,8 +456,8 @@
         ratio = std_cond / std_guided
         guided = guided_v[p]
         velocity = rescale_mix * ratio * guided + (1.0 - rescale_mix) * guided
-        velocity_out[p] = velocity
-        latent_out[p] = latent[p] + delta * velocity
+        results[0, p] = velocity
+        results[1, p] = latent[p] + delta * velocity
 
 
 def body(
@@ -465,20 +489,23 @@
     hidden_own = expand_weight.shape[0]
     per_seq = n // batch
     rows = batch * img_local
-    bias_row = jnp.pad(expand_bias.astype(f32), (0, LANES - hidden_own)).reshape(1, LANES)
-    vmem = pl.BlockSpec(memory_space=pltpu.VMEM)
-    smem = pl.BlockSpec(memory_space=pltpu.SMEM)
     hbm = pl.BlockSpec(memory_space=pl.ANY)
     dma = pltpu.SemaphoreType.DMA
     half = n // 4
-    return pl.pallas_call(
+    arrays = (
+        img_query, img_key, img_value, txt_key, txt_value, expand_bias, txt_len,
+        slot_of, step_index, residual, modulation.transpose(1, 0, 2), out_weight, out_bias, contract_bias,
+        final_weight.T, final_bias, latent,
+    )
+    held = tuple((pltpu.SMEM if a.dtype == jnp.int32 else pltpu.VMEM)(a.shape, a.dtype) for a in arrays)
+    results = pl.pallas_call(
         functools.partial(kernel, (groups, n, y_size, per_seq)),
-        out_shape=(jax.ShapeDtypeStruct(latent.shape, f32), jax.ShapeDtypeStruct(latent.shape, f32)),
-        in_specs=[smem] * 3 + [vmem] * 7 + [hbm, vmem, hbm, vmem, hbm] + [vmem] * 4,
-        out_specs=(vmem, vmem),
+        out_shape=jax.ShapeDtypeStruct((2, *latent.shape), f32),
+        in_specs=[hbm, hbm, tuple(hbm for _ in arrays)],
+        out_specs=pl.BlockSpec(memory_space=pltpu.VMEM),
         scratch_shapes=[
+            held,
             pltpu.VMEM((4, 2, n, hidden_own, d_model // 4), bf16),
-            pltpu.VMEM((d_model, d_model), bf16),
             pltpu.VMEM((ITEMS, n, 16, LANES), bf16),
             pltpu.VMEM((ITEMS, n, 16, LANES), bf16),
             pltpu.VMEM((ITEMS, n, 4, LANES), bf16),
@@ -493,7 +520,7 @@
             pltpu.VMEM((rows, d_model), f32),
             pltpu.VMEM((batch, img_local, PATCH), f32),
             pltpu.VMEM((prompts, img_local, PATCH), f32),
-            dma((1,)),
+            dma((len(arrays),)),
             dma((4, 2)),
             dma((ITEMS,)),
             dma((ITEMS,)),
@@ -518,12 +545,8 @@
         compiler_params=pltpu.CompilerParams(
             collective_id=0, has_side_effects=True, vmem_limit_bytes=60 * 1024 * 1024
         ),
-    )(
-        txt_len, slot_of, step_index,
-        img_query, img_key, img_value, txt_key, txt_value,
-        residual, modulation, out_weight, out_bias.reshape(1, -1), expand_weight, bias_row,
-        contract_weight, contract_bias.reshape(1, -1), final_weight, final_bias.reshape(1, -1), latent,
-    )
+    )(expand_weight, contract_weight, arrays)
+    return results[0], results[1]
 
 
 def solution(mesh):

time: 215 us -> 186 us (0.87)
  Pallas kernels: 203 us -> 183 us
  local copies, waits for them, and re-layouts: 8.96 us -> 1.35 us
    pallas_call x1, Pallas kernels: 203 us -> 183 us  [body(): pl.pallas_call(functools.partial(kernel, (groups, n, y_size, per_seq)), o...]
    unnamed x4 -> x0, local copies, waits for them, and re-layouts: 6.37 us -> none
    reshape x2 -> x0, local copies, waits for them, and re-layouts: 2.59 us -> none  [the longest x1 1.29 us: body(): out_bias.reshape(1, -1)]
where the time goes in v2:
time: 186 us
  Pallas kernels  183 us (98%)
    pallas_call x1, Pallas kernels, body(): pl.pallas_call(functools.partial(kernel, (groups, n, y_size, per_seq)), o...  183 us

profile of v2, /device:TPU:37, one launch (start us, length us, event | category | flops | bytes accessed | tf_op | source)
XLA Modules:
  0.0 185.7 jit_solution(9056741185960688438)
XLA Ops:
  1.3 183.0 %shard_map.194 = f32[2,4,8,64]{3,2,1,0:T(8,128)} custom-call(bf16[48,1536]{1,0:T(8,128)(2,1)} %expand_weight.1, bf16[48,1536]{1,0:T(8,128)(2,1)} %contract_weight.1, bf16[8,8,1536]{2,1,0:T(8,128)(2,1)} %arrays_0_.1, bf16[8,8,1536]{2,1,0:T(8,128)(2,1)} %arrays_1_.1, bf16[8,8,1536]{2,1,0:T(8,128)(2,1)} %arrays_2_.1, bf16[8,4,1536]{2,1,0:T(4,128)(2,1)} %arrays_3_.1, ...), custom_call_target="tpu_custom_call" | custom-call | tf_op jit(solution)/shard_map/pallas_call | solution.py:501
  184.3 1.3 slice_bitcast_fusion

commit v3 on v2

--- a/solution.py
+++ b/solution.py
@@ -48,7 +48,7 @@
     expand_weight, contract_weight, arrays, results, held,
     wall, pack, got, outb, back, attended, bias_all, bias_rows, bias_units, sums_all, hidden, ff_in, acc, pred_v, guided_v,
     in_sem, w_sem, qkv_send, qkv_recv, ret_send, ret_recv, own_recv, x_recv, y_recv, d_recv, sib_recv,
-    ring_send, sib_send, x_send, y_send, xr_send, yr_send, bias_send, bias_recv, sums_send, sums_recv,
+    ring_send, sib_send, x_send, y_send, xr_send, yr_send, bias_send, bias_recv, bias_sib_send, bias_sib_recv, sums_send, sums_recv,
 ):
     groups, n, y_size, per_seq = sizes
     (
@@ -76,8 +76,12 @@
 
     barrier = pltpu.get_barrier_semaphore()
 
+    def peer_at(j):
+        away = n // 2 + (1 - 2 * (j % 2)) * (j // 2)
+        return me + away - n * (me + away >= n).astype(jnp.int32)
+
     def greet(j, c):
-        pl.semaphore_signal(barrier, inc=1, device_id=(g, lax.rem(me + j, n)), device_id_type=MESH)
+        pl.semaphore_signal(barrier, inc=1, device_id=(g, peer_at(j)), device_id_type=MESH)
         return c
 
     lax.fori_loop(1, n, greet, 0)
@@ -154,9 +158,6 @@
 
     scope = jax.named_scope
 
-    def offset(j):
-        return jnp.where(lax.rem(j, 2) == 0, n // 2 + j // 2, n // 2 - j // 2)
-
     def ring(slot, direction, k, to):
         return pltpu.make_async_remote_copy(
             wall.at[q, :, slot], wall.at[q, :, slot], ring_send.at[direction], own_recv.at[direction, k],
@@ -180,22 +181,29 @@
             return lax.rem(me + n - 2 * k, n)
         return lax.rem(me + 2 * k, n)
 
+    def bias_ring(slot, direction, k, to):
+        return pltpu.make_async_remote_copy(
+            bias_all.at[slot], bias_all.at[slot], bias_send.at[direction], bias_recv.at[direction, k],
+            device_id=(g, to), device_id_type=MESH,
+        )
+
+    def bias_sibling(slot):
+        return pltpu.make_async_remote_copy(
+            bias_all.at[slot], bias_all.at[slot], bias_sib_send, bias_sib_recv,
+            device_id=(g, sibling), device_id_type=MESH,
+        )
+
+    bias_ring(me, 0, 1, right).start()
+    bias_ring(me, 1, 1, left).start()
+    bias_sibling(me).start()
     ring(me, 0, 1, right).start()
     ring(me, 1, 1, left).start()
     for part in range(4):
         to_sibling(part, me).start()
 
-    def send_bias(j, c):
-        peer = lax.rem(me + offset(j), n)
-        pltpu.make_async_remote_copy(
-            bias_all.at[me], bias_all.at[me], bias_send, bias_recv,
-            device_id=(g, peer), device_id_type=MESH,
-        ).start()
-        return c
-
     def send_item(index, c):
-        i = index // (n - 1)
-        peer = lax.rem(me + offset(lax.rem(index, n - 1) + 1), n)
+        i = sum((index >= at * (n - 1)).astype(jnp.int32) for at in range(1, ITEMS))
+        peer = peer_at(index - i * (n - 1) + 1)
         pltpu.make_async_remote_copy(
             pack.at[i, peer], got.at[i, me], qkv_send.at[i], qkv_recv.at[i],
             device_id=(g, peer), device_id_type=MESH,
@@ -250,7 +258,7 @@
         outb[i] = jnp.stack([both[:, 0:4], both[:, 4:8]], axis=1).reshape(n, 4, LANES)
 
         def send_back(j, carry):
-            peer = lax.rem(me + offset(j), n)
+            peer = peer_at(j)
             pltpu.make_async_remote_copy(
                 outb.at[i, peer], back.at[i, me], ret_send.at[i], ret_recv.at[i],
                 device_id=(g, peer), device_id_type=MESH,
@@ -269,10 +277,6 @@
             with scope("send"):
                 lax.fori_loop(first, jnp.minimum(first + SENDS_PER_STEP, total), send_item, 0)
 
-        @pl.when(k == 4)
-        def _():
-            lax.fori_loop(1, n, send_bias, 0)
-
         for direction, last, onward in ((0, half, right), (1, half - 1, left)):
 
             @pl.when(k <= last)
@@ -280,14 +284,17 @@
                 slot = slot_at(direction, k)
                 with scope("own"):
                     ring(slot, direction, k, onward).wait_recv()
+                    bias_ring(slot, direction, k, onward).wait_recv()
 
                 @pl.when(k < last)
                 def _():
                     ring(slot, direction, k + 1, onward).start()
+                    bias_ring(slot, direction, k + 1, onward).start()
 
                 across(q, slot, x_send, x_recv.at[direction, k], x_partner).start()
                 across(q, slot, y_send, y_recv.at[direction, k], y_partner).start()
                 to_sibling(q, slot).start()
+                bias_sibling(slot).start()
 
         for direction, last in ((0, half), (1, half - 1)):
             late = k - LAG
@@ -329,7 +336,7 @@
     chunks = len(range(0, n, CHUNK))
     hidden_own = wall.shape[3]
     chunk_units = CHUNK * hidden_own
-    drain(bias_all.at[pl.ds(0, n - 1)], bias_recv)
+    drain(bias_all.at[pl.ds(0, chips)], bias_sib_recv)
     for r in range(n):
         bias_rows[r : r + 1, :] = bias_all[r]
     unit = lax.broadcasted_iota(jnp.int32, (LANES, chunk_units), 1)
@@ -367,29 +374,30 @@
         .reshape(batch * img_local, d_model)
         .astype(bf16)
     )
-    acc[...] = jnp.zeros_like(acc)
-
     for part in range(4):
         with scope("sib"):
             drain(wall.at[part, :, pl.ds(0, chips)], sib_recv.at[part])
 
-    def feed(c, carry):
+    for c in range(chunks):
         blocks = pl.ds(c * CHUNK, CHUNK)
         pre = bias_units[c]
-        for part in range(4):
-            w = wall[part, 0, blocks].reshape(chunk_units, width)
+        for side in range(2):
+            w = jnp.concatenate(
+                [wall[part, 0, blocks].reshape(chunk_units, width) for part in (2 * side, 2 * side + 1)], axis=1
+            )
             pre = pre + lax.dot_general(
-                ff_in[:, part * width : (part + 1) * width], w,
+                ff_in[:, 2 * side * width : 2 * (side + 1) * width], w,
                 (((1,), (1,)), ((), ())), preferred_element_type=f32,
             )
         act = (0.5 * pre * (1.0 + jnp.tanh(math.sqrt(2.0 / math.pi) * (pre + 0.044715 * pre * pre * pre)))).astype(bf16)
-        for part in range(4):
-            w = wall[part, 1, blocks].reshape(chunk_units, width)
-            acc[:, part * width : (part + 1) * width] += jnp.dot(act, w, preferred_element_type=f32)
-        return carry
-
-    with scope("ffn"):
-        lax.fori_loop(0, chunks, feed, 0)
+        for side in range(2):
+            w = jnp.concatenate(
+                [wall[part, 1, blocks].reshape(chunk_units, width) for part in (2 * side, 2 * side + 1)], axis=1
+            )
+            columns = slice(2 * side * width, 2 * (side + 1) * width)
+            product = jnp.dot(act, w, preferred_element_type=f32)
+            acc[:, columns] = product if c == 0 else acc[:, columns] + product
+
 
     ff_hidden = hidden[...] + modulation[3][:, None, :] * (acc[...].reshape(shape3) + contract_bias[...].reshape(1, 1, -1))
     normed = (
@@ -418,7 +426,7 @@
     sums_all[me] = row
 
     def send_sums(j, c):
-        peer = lax.rem(me + offset(j), n)
+        peer = peer_at(j)
         pltpu.make_async_remote_copy(
             sums_all.at[me], sums_all.at[me], sums_send, sums_recv,
             device_id=(g, peer), device_id_type=MESH,
@@ -427,8 +435,9 @@
 
     lax.fori_loop(1, n, send_sums, 0)
 
-    with scope("left"):
-        pass
+    values = float(img_local * n * PATCH)
+    step_float = jnp.full((img_local, PATCH), step_index[0], jnp.int32).astype(f32)
+    delta = sigma_at(1.0 - (step_float + 1.0) / NSTEPS) - sigma_at(1.0 - step_float / NSTEPS)
     for direction, count in ((0, half), (1, half - 1)):
         drain(wall.at[0, :, pl.ds(0, count)], ring_send.at[direction])
     for part in range(4):
@@ -437,7 +446,9 @@
     drain(wall.at[0, :, pl.ds(0, chips - 1)], y_send)
     drain(wall.at[0, :, pl.ds(0, half - 1)], xr_send)
     drain(wall.at[0, :, pl.ds(0, half)], yr_send)
-    drain(bias_all.at[pl.ds(0, n - 1)], bias_send)
+    for direction, count in ((0, half), (1, half - 1)):
+        drain(bias_all.at[pl.ds(0, count)], bias_send.at[direction])
+    drain(bias_all.at[pl.ds(0, chips)], bias_sib_send)
     for i in range(ITEMS):
         drain(pack.at[i, pl.ds(0, n - 1)], qkv_send.at[i])
         drain(outb.at[i, pl.ds(0, n - 1)], ret_send.at[i])
@@ -446,13 +457,10 @@
     drain(sums_all.at[pl.ds(0, n - 1)], sums_send)
 
     totals = jnp.sum(sums_all[...], axis=0)
-    count = float(img_local * n * PATCH)
-    step_float = jnp.full((img_local, PATCH), step_index[0], jnp.int32).astype(f32)
-    delta = sigma_at(1.0 - (step_float + 1.0) / NSTEPS) - sigma_at(1.0 - step_float / NSTEPS)
     for p in range(prompts):
         t = [totals[:, s * prompts + p : s * prompts + p + 1] for s in range(4)]
-        std_cond = jnp.sqrt((t[1] - t[0] * t[0] / count) / (count - 1.0) + 1e-06)
-        std_guided = jnp.sqrt((t[3] - t[2] * t[2] / count) / (count - 1.0) + 1e-06)
+        std_cond = jnp.sqrt((t[1] - t[0] * t[0] / values) / (values - 1.0) + 1e-06)
+        std_guided = jnp.sqrt((t[3] - t[2] * t[2] / values) / (values - 1.0) + 1e-06)
         ratio = std_cond / std_guided
         guided = guided_v[p]
         velocity = rescale_mix * ratio * guided + (1.0 - rescale_mix) * guided
@@ -537,6 +545,8 @@
             dma,
             dma,
             dma,
+            dma((2,)),
+            dma((2, half + 1)),
             dma,
             dma,
             dma,

time: 186 us -> 184 us (0.989)
  Pallas kernels: 183 us -> 181 us
where the time goes in v3:
time: 184 us
  Pallas kernels  181 us (98%)
    pallas_call x1, Pallas kernels, body(): pl.pallas_call(functools.partial(kernel, (groups, n, y_size, per_seq)), o...  181 us

profile of v3, /device:TPU:37, one launch (start us, length us, event | category | flops | bytes accessed | tf_op | source)
XLA Modules:
  0.0 184.0 jit_solution(10882724939972729874)
XLA Ops:
  1.3 181.3 %shard_map.194 = f32[2,4,8,64]{3,2,1,0:T(8,128)} custom-call(bf16[48,1536]{1,0:T(8,128)(2,1)} %expand_weight.1, bf16[48,1536]{1,0:T(8,128)(2,1)} %contract_weight.1, bf16[8,8,1536]{2,1,0:T(8,128)(2,1)} %arrays_0_.1, bf16[8,8,1536]{2,1,0:T(8,128)(2,1)} %arrays_1_.1, bf16[8,8,1536]{2,1,0:T(8,128)(2,1)} %arrays_2_.1, bf16[8,4,1536]{2,1,0:T(4,128)(2,1)} %arrays_3_.1, ...), custom_call_target="tpu_custom_call" | custom-call | tf_op jit(solution)/shard_map/pallas_call | solution.py:509
  182.6 1.3 slice_bitcast_fusion
